TPU v7x, 64 devices: a 2x2x8 block of a 4x4x8 slice. The times are simulated.
64 devices in a mesh: dp: 8 (over x, y, core), tp: 8 (over z).
Axes of the slice: x: 2, y: 2, z: 8, core: 2. Of those that a mesh axis runs over, the one named last changes fastest.
The devices are a block of a 4x4x8 slice.
Arguments:
- x: bfloat16 [16384, 2048], P('dp'), parts along dimension 0
- dy: bfloat16 [16384, 2048], P('dp'), parts along dimension 0
- gate: bfloat16 [16384, 8192], P('dp', 'tp'), parts along dimension 0
- up: bfloat16 [16384, 8192], P('dp', 'tp'), parts along dimension 0
- w_gate: bfloat16 [2048, 8192], P(None, 'tp')
- w_up: bfloat16 [2048, 8192], P(None, 'tp')
- w_down: bfloat16 [8192, 2048], P('tp')
Outputs:
- output 1: bfloat16 [16384, 2048], P('dp'), parts along dimension 0
- output 2: bfloat16 [16384, 8192], P('dp', 'tp'), parts along dimension 0
- output 3: bfloat16 [16384, 8192], P('dp', 'tp'), parts along dimension 0
- output 4: bfloat16 [65536, 2048], P(('dp', 'tp')), parts along dimension 0
There are 8 independent parts. A program takes and returns all parts, laid end to end along the dimension named above; an argument that names none is the same for every part.
All inputs are finite; a program needn't handle non-finite values.
Results may differ from a plain program's by a relative error of at most 0.012.
Values are sent between devices in bfloat16 or wider.
A program may use at most 768 MiB of HBM per device.

v0:
```python
import jax
import jax.numpy as jnp
from jax import lax
from jax.sharding import PartitionSpec as P


def act(gate, up):
    return jax.nn.silu(gate) * up


def solution(mesh):
    def step(x, dy, gate, up, w_gate, w_up, w_down):
        hidden, back = jax.vjp(act, gate.astype(jnp.float32), up.astype(jnp.float32))
        d_hidden = jnp.dot(dy, w_down.T, preferred_element_type=jnp.float32)
        d_gate, d_up = (g.astype(jnp.bfloat16) for g in back(d_hidden))
        term = jnp.dot(d_gate, w_gate.T, preferred_element_type=jnp.float32) + jnp.dot(d_up, w_up.T, preferred_element_type=jnp.float32)
        dx = lax.psum(term.astype(jnp.bfloat16), "tp")
        dw_gate = jnp.dot(x.T, d_gate, preferred_element_type=jnp.float32)
        dw_up = jnp.dot(x.T, d_up, preferred_element_type=jnp.float32)
        dw_down = jnp.dot(hidden.astype(jnp.bfloat16).T, dy, preferred_element_type=jnp.float32)
        return dx, *(g.astype(jnp.bfloat16) for g in (dw_gate, dw_up, dw_down))

    tokens, columns, rows = P("dp", None), P(None, "tp"), P("tp", None)
    return jax.shard_map(
        step,
        mesh=mesh,
        in_specs=(tokens, tokens, P("dp", "tp"), P("dp", "tp"), columns, columns, rows),
        out_specs=(tokens, P("dp", "tp"), P("dp", "tp"), P(("dp", "tp"), None)),
        check_vma=False,
    )
```

profile of v0, /device:TPU:21, one launch (start us, length us, event | category | flops | bytes accessed | tf_op | source)
XLA Modules:
  0.0 260.8 jit_solution(3095499455458105641)
XLA Ops:
  7.2 0.1 all-reduce.2.cloned.1.call-start
  7.2 0.0 copy-start
  7.3 20.2 %fusion.6 = (bf16[2048,1024]{1,0:T(8,128)(2,1)S(1)}, f32[2048,1024]{1,0:T(8,128)}) fusion(bf16[2048,1024]{1,0:T(8,128)(2,1)} %param.9, bf16[2048,1024]{1,0:T(8,128)(2,1)} %param.10, bf16[2048,2048]{1,0:T(8,128)(2,1)} %param.8, bf16[1024,2048]{1,0:T(8,128)(2,1)} %param.13), kind=kOutput, calls=%fused_computation.13 | convolution fusion | flops 8617197568 | bytes 33554432 | tf_op jit(solution)/shard_map/dot_general | solution.py:14
  27.5 0.0 copy-start.1
  27.5 0.0 copy-done
  27.5 11.8 %fusion.13 = f32[2048,2048]{1,0:T(8,128)} fusion(bf16[2048,1024]{1,0:T(8,128)(2,1)S(1)} %get-tuple-element.8, bf16[2048,1024]{1,0:T(8,128)(2,1)S(1)} %copy-done), kind=kOutput, calls=%fused_computation.20 | convolution fusion | flops 8589934592 | bytes 25165824 | tf_op jit(solution)/shard_map/dot_general | solution.py:16
  39.2 0.0 copy-done.1
  39.2 20.5 %add_convert_fusion = bf16[2048,2048]{1,0:T(8,128)(2,1)} fusion(f32[2048,2048]{1,0:T(8,128)} %fusion.13, bf16[2048,1024]{1,0:T(8,128)(2,1)} %param.12, f32[2048,1024]{1,0:T(8,128)} %get-tuple-element.9, bf16[2048,1024]{1,0:T(8,128)(2,1)} %param.9), kind=kOutput, calls=%fused_computation | convolution fusion | flops 8613003264 | bytes 41943040 | tf_op jit(solution)/shard_map/dot_general | solution.py:16
  59.7 0.1 all-reduce.2.cloned.1.call-update
  59.8 14.0 %convert_bitcast_fusion.1 = bf16[2048,1024]{0,1:T(8,128)(2,1)} fusion(bf16[2048,1024]{1,0:T(8,128)(2,1)} %copy-done.1, bf16[2048,2048]{1,0:T(8,128)(2,1)} %param.7), kind=kOutput, calls=%fused_computation.17 | convolution fusion | flops 8592031744 | bytes 16777216 | tf_op jit(solution)/shard_map/dot_general | solution.py:18
  73.8 6.4 %copy.11 = bf16[2048,1024]{1,0:T(8,128)(2,1)} copy(bf16[2048,1024]{0,1:T(8,128)(2,1)} %convert_bitcast_fusion.1) | data formatting | bytes 8388608
  80.2 16.4 %convert_bitcast_fusion = bf16[2048,1024]{0,1:T(8,128)(2,1)} fusion(bf16[2048,2048]{1,0:T(8,128)(2,1)} %param.7, f32[2048,1024]{1,0:T(8,128)} %get-tuple-element.9, bf16[2048,1024]{1,0:T(8,128)(2,1)} %param.9), kind=kOutput, calls=%fused_computation.16 | convolution fusion | flops 8606711808 | bytes 25165824 | tf_op jit(solution)/shard_map/dot_general | solution.py:19
  96.6 6.4 %copy.12 = bf16[2048,1024]{1,0:T(8,128)(2,1)} copy(bf16[2048,1024]{0,1:T(8,128)(2,1)} %convert_bitcast_fusion) | data formatting | bytes 8388608
  103.0 16.2 %fusion.9 = bf16[1024,2048]{1,0:T(8,128)(2,1)} fusion(bf16[2048,2048]{1,0:T(8,128)(2,1)} %param.8, bf16[2048,1024]{1,0:T(8,128)(2,1)} %param.10, bf16[2048,1024]{1,0:T(8,128)(2,1)} %param.9), kind=kOutput, calls=%fused_computation.18 | convolution fusion | flops 8608808960 | bytes 20971520 | tf_op jit(solution)/shard_map/dot_general | solution.py:20
  119.3 126.3 %all-reduce.2.cloned.1.call-done = bf16[2048,2048]{1,0:T(8,128)(2,1)} async-done(((bf16[2048,2048]{1,0:T(8,128)(2,1)}), bf16[2048,2048]{1,0:T(8,128)(2,1)}) %all-reduce.2.cloned.1.call-update) | async-done | bytes 8388624 | tf_op jit(solution)/shard_map/psum | solution.py:17
  245.5 8.4 %copy.14 = bf16[2048,2048]{1,0:T(8,128)(2,1)} copy(bf16[2048,2048]{1,0:T(8,128)(2,1)} %all-reduce.2.cloned.1.call-done) | data formatting | bytes 16777216
Async XLA Ops:
  7.2 238.4 %all-reduce.2.cloned.1.call-start = ((), (), s32[]{:S(2)}) async-start(), calls=%async_computation | async-start | bytes 16777216 | tf_op jit(solution)/shard_map/psum | solution.py:17
  7.2 20.2 %copy-start = (bf16[2048,1024]{1,0:T(8,128)(2,1)S(1)}, bf16[2048,1024]{1,0:T(8,128)(2,1)}, u32[]{:S(2)}) copy-start(bf16[2048,1024]{1,0:T(8,128)(2,1)} %param.11) | copy-start | bytes 12582916
  27.5 11.8 %copy-start.1 = (bf16[2048,1024]{1,0:T(8,128)(2,1)}, bf16[2048,1024]{1,0:T(8,128)(2,1)S(1)}, u32[]{:S(2)}) copy-start(bf16[2048,1024]{1,0:T(8,128)(2,1)S(1)} %get-tuple-element.8) | copy-start | bytes 12582916
Sparse Core Ops, SparseCore 0:
  59.9 185.5 all-reduce.1
where the time goes:
time: 261 us
  waiting for transfers between devices  126 us (48%)
  matrix products  99.1 us (38%)
  local copies, waits for them, and re-layouts  21.2 us (8%)
  between operations  14.1 us (5%)
    psum x1, waiting for transfers between devices, step(): dx = lax.psum(term.astype(jnp.bfloat16), 'tp')  126 us
    unnamed x7, local copies, waits for them, and re-layouts  21.2 us
    dot_general x1, matrix products, step(): jnp.dot(d_up, w_up.T, preferred_element_type=jnp.float32)  20.5 us
    dot_general x1, matrix products, step(): d_hidden = jnp.dot(dy, w_down.T, preferred_element_type=jnp.float32)  20.2 us
    dot_general x1, matrix products, step(): dw_up = jnp.dot(x.T, d_up, preferred_element_type=jnp.float32)  16.4 us
    dot_general x1, matrix products, step(): jnp.dot(hidden.astype(jnp.bfloat16).T, dy, preferred_element_type=jnp.flo...  16.2 us
    dot_general x1, matrix products, step(): dw_gate = jnp.dot(x.T, d_gate, preferred_element_type=jnp.float32)  14 us
    dot_general x1, matrix products, step(): jnp.dot(d_gate, w_gate.T, preferred_element_type=jnp.float32)  11.8 us
  transfers between devices with their start and end apart: 1, of which 1 were waited for; matrix products, arithmetic and copies ran while one was open for 23% of the time, Pallas kernels for 0%

commit v1 on v0

v1 whole, which is shorter than its diff:
```python
import functools

import jax
import jax.numpy as jnp
from jax import lax
from jax.experimental import pallas as pl
from jax.experimental.pallas import tpu as pltpu
from jax.sharding import PartitionSpec as P

RINGS = 8
CHUNKS = 4
TILE = 128
BF16, F32 = jnp.bfloat16, jnp.float32
NT = (((1,), (1,)), ((), ()))
TN = (((0,), (0,)), ((), ()))


def kernel(
    n,
    x,
    dy,
    gate,
    up,
    w_gate,
    w_up,
    w_down,
    dx,
    dw_gate,
    dw_up,
    dw_down,
    x_v,
    dy_v,
    dg_v,
    du_v,
    hid_v,
    wg_v,
    wu_v,
    wd_v,
    dx_v,
    slots,
    stage,
    in_sem,
    wd_sem,
    w_sem,
    x_sem,
    stage_sem,
    dx_sem,
    send_sem,
    rs_sem,
    ag_sem,
):
    tokens, depth = dy.shape
    hidden = gate.shape[1]
    rows, cols, fcols = tokens // n, depth // RINGS, hidden // CHUNKS
    me = lax.axis_index("tp")
    right, left = lax.rem(me + 1, n), lax.rem(me + n - 1, n)

    barrier = pltpu.get_barrier_semaphore()
    for neighbour in (left, right):
        pl.semaphore_signal(barrier, inc=1, device_id={"tp": neighbour}, device_id_type=pl.DeviceIdType.MESH)

    def block(b):
        return pl.ds(pl.multiple_of(b * rows, rows), rows)

    def strip(s):
        return pl.ds(pl.multiple_of(s * cols, cols), cols)

    def chunk(c):
        return pl.ds(pl.multiple_of(c * fcols, fcols), fcols)

    def tile(i):
        return pl.ds(pl.multiple_of(i * TILE, TILE), TILE)

    def rows_in(b):
        return [
            pltpu.make_async_copy(src.at[block(b), :], dst.at[block(b), :], in_sem.at[k, b])
            for k, (src, dst) in enumerate(((dy, dy_v), (gate, dg_v), (up, du_v)))
        ]

    def down_in(c):
        return pltpu.make_async_copy(w_down.at[chunk(c), :], wd_v.at[chunk(c), :], wd_sem.at[c])

    def strips_in(s):
        return [
            pltpu.make_async_copy(src.at[strip(s), :], dst.at[strip(s), :], w_sem.at[k, s])
            for k, (src, dst) in enumerate(((w_gate, wg_v), (w_up, wu_v)))
        ]

    x_in = pltpu.make_async_copy(x, x_v, x_sem)

    def right_block(t):
        return lax.rem(me + 2 * n - 1 - t, n)

    def left_block(t):
        return lax.rem(me + n - 1 + t, n)

    for copy in rows_in(right_block(0)):
        copy.start()
    for c in range(CHUNKS):
        down_in(c).start()

    @pl.loop(0, RINGS)
    def _(s):
        for copy in strips_in(s):
            copy.start()

    @pl.loop(1, n // 2)
    def _(t):
        for copy in rows_in(right_block(t)) + rows_in(left_block(t)):
            copy.start()

    for copy in rows_in(left_block(n // 2)):
        copy.start()
    x_in.start()

    def grads(b, c):
        at = (block(b), chunk(c))
        d_hidden = lax.dot_general(dy_v[block(b), :], wd_v[chunk(c), :], NT, preferred_element_type=F32)
        g, u = dg_v[at].astype(F32), du_v[at].astype(F32)
        sig = jax.nn.sigmoid(g)
        act = g * sig
        hid_v[at] = (act * u).astype(BF16)
        dg_v[at] = (d_hidden * u * (sig + act * (1.0 - sig))).astype(BF16)
        du_v[at] = (d_hidden * act).astype(BF16)

    def term(b, s):
        return lax.dot_general(dg_v[block(b), :], wg_v[strip(s), :], NT, preferred_element_type=F32) + lax.dot_general(
            du_v[block(b), :], wu_v[strip(s), :], NT, preferred_element_type=F32
        )

    def target(odd):
        return {"tp": left if odd else right}

    def rs_copy(s, odd, t):
        return pltpu.make_async_remote_copy(
            src_ref=slots.at[s, t],
            dst_ref=slots.at[s, t + 1],
            send_sem=send_sem.at[s],
            recv_sem=rs_sem.at[s, t],
            device_id=target(odd),
            device_id_type=pl.DeviceIdType.MESH,
        )

    def ag_block(odd, t):
        return lax.rem(me + n - 2 + t, n) if odd else lax.rem(me + n - t, n)

    def ag_copy(s, odd, t):
        here = dx_v.at[block(ag_block(odd, t)), strip(s)]
        return pltpu.make_async_remote_copy(
            src_ref=here,
            dst_ref=here,
            send_sem=send_sem.at[s],
            recv_sem=ag_sem.at[s, t],
            device_id=target(odd),
            device_id_type=pl.DeviceIdType.MESH,
        )

    def dx_out(s, odd, t):
        at = (block(ag_block(odd, t)), strip(s))
        return pltpu.make_async_copy(dx_v.at[at], dx.at[at], dx_sem)

    def send_first(s, odd):
        slots[s, 0] = term(right_block(0), s).astype(BF16)
        rs_copy(s, odd, 0).start()

    def pass_on(s, odd, t):
        rs_copy(s, odd, t - 1).wait_recv()
        b = left_block(t) if odd else right_block(t)
        slots[s, t] = (slots[s, t].astype(F32) + term(b, s)).astype(BF16)
        rs_copy(s, odd, t - 1).wait_send()
        rs_copy(s, odd, t).start()

    def finish(s, odd):
        t = n - 1
        rs_copy(s, odd, t - 1).wait_recv()
        b = left_block(t) if odd else right_block(t)
        dx_v[block(b), strip(s)] = (slots[s, t].astype(F32) + term(b, s)).astype(BF16)
        rs_copy(s, odd, t - 1).wait_send()
        ag_copy(s, odd, 0).start()
        dx_out(s, odd, 0).start()

    def hand_on(s, odd, t, last=False):
        before = t - 1
        arrived = pltpu.make_async_remote_copy(
            src_ref=dx_v.at[block(ag_block(odd, t)), strip(s)],
            dst_ref=dx_v.at[block(ag_block(odd, t)), strip(s)],
            send_sem=send_sem.at[s],
            recv_sem=ag_sem.at[s, before],
            device_id=target(odd),
            device_id_type=pl.DeviceIdType.MESH,
        )
        arrived.wait_recv()
        arrived.wait_send()
        if not last:
            ag_copy(s, odd, t).start()
        dx_out(s, odd, t).start()

    def stage_copies(i, slot, targets):
        width = stage.shape[-1] // len(targets)
        return [
            pltpu.make_async_copy(
                stage.at[slot, :, pl.ds(k * width, width)], dst.at[tile(i), :], stage_sem.at[k, slot]
            )
            for k, dst in enumerate(targets)
        ]

    def down_grad(i):
        slot = lax.rem(i, 2)

        @pl.when(i >= 2)
        def _():
            for copy in stage_copies(i - 2, slot, [dw_down]):
                copy.wait()

        stage[slot] = lax.dot_general(hid_v[:, tile(i)], dy_v[...], TN, preferred_element_type=F32).astype(BF16)
        for copy in stage_copies(i, slot, [dw_down]):
            copy.start()

    def up_grads(i):
        slot = lax.rem(i, 2)

        @pl.when(i >= 2)
        def _():
            for copy in stage_copies(i - 2, slot, [dw_gate, dw_up]):
                copy.wait()

        xt = x_v[:, tile(i)]
        stage[slot, :, :hidden] = lax.dot_general(xt, dg_v[...], TN, preferred_element_type=F32).astype(BF16)
        stage[slot, :, hidden:] = lax.dot_general(xt, du_v[...], TN, preferred_element_type=F32).astype(BF16)
        for copy in stage_copies(i, slot, [dw_gate, dw_up]):
            copy.start()

    for copy in rows_in(right_block(0)):
        copy.wait()

    @pl.loop(0, CHUNKS)
    def _(c):
        down_in(c).wait()
        grads(right_block(0), c)

    pl.semaphore_wait(barrier, 2)
    pairs = RINGS // 2
    per_pair = 2 * CHUNKS // pairs

    @pl.loop(0, pairs)
    def _(j):
        for odd in range(2):
            for copy in strips_in(2 * j + odd):
                copy.wait()
            send_first(2 * j + odd, odd)

    def arrive(b):
        for copy in rows_in(b):
            copy.wait()

    arrive(right_block(1))

    @pl.loop(0, CHUNKS)
    def _(c):
        grads(right_block(1), c)

    arrive(left_block(1))

    @pl.loop(0, CHUNKS)
    def _(c):
        grads(left_block(1), c)

    half = n // 2

    @pl.loop(1, half - 1)
    def _(t):
        arrive(right_block(t + 1))
        arrive(left_block(t + 1))

        @pl.loop(0, pairs)
        def _(j):
            pass_on(2 * j, 0, t)
            grads(right_block(t + 1), j)
            pass_on(2 * j + 1, 1, t)
            grads(left_block(t + 1), j)

    arrive(left_block(half))

    @pl.loop(0, pairs)
    def _(j):
        pass_on(2 * j, 0, half - 1)
        grads(left_block(half), j)
        pass_on(2 * j + 1, 1, half - 1)

    @pl.loop(half, n - 1)
    def _(t):
        @pl.loop(0, pairs)
        def _(j):
            pass_on(2 * j, 0, t)
            pass_on(2 * j + 1, 1, t)
            i = (t - half) * pairs + j

            @pl.when(i < hidden // TILE)
            def _():
                down_grad(i)

    for i in range(hidden // TILE - 2, hidden // TILE):
        for copy in stage_copies(i, i % 2, [dw_down]):
            copy.wait()
    x_in.wait()

    @pl.loop(0, pairs)
    def _(j):
        finish(2 * j, 0)
        finish(2 * j + 1, 1)

    @pl.loop(1, n - 1)
    def _(t):
        @pl.loop(0, pairs)
        def _(j):
            hand_on(2 * j, 0, t)
            hand_on(2 * j + 1, 1, t)
            i = (t - 1) * pairs + j

            @pl.when(i < depth // TILE)
            def _():
                up_grads(i)

    for i in range(depth // TILE - 2, depth // TILE):
        for copy in stage_copies(i, i % 2, [dw_gate, dw_up]):
            copy.wait()

    @pl.loop(0, pairs)
    def _(j):
        hand_on(2 * j, 0, n - 1, last=True)
        hand_on(2 * j + 1, 1, n - 1, last=True)

    pltpu.make_async_copy(dx_v, dx, dx_sem).wait()


def solution(mesh):
    n = mesh.shape["tp"]

    def step(x, dy, gate, up, w_gate, w_up, w_down):
        tokens, depth = dy.shape
        hidden = gate.shape[1]
        rows, cols = tokens // n, depth // RINGS
        hbm = pl.BlockSpec(memory_space=pltpu.HBM)
        dma = pltpu.SemaphoreType.DMA
        return pl.pallas_call(
            functools.partial(kernel, n),
            name="mlp_backward",
            out_shape=[
                jax.ShapeDtypeStruct((tokens, depth), BF16),
                jax.ShapeDtypeStruct((depth, hidden), BF16),
                jax.ShapeDtypeStruct((depth, hidden), BF16),
                jax.ShapeDtypeStruct((hidden, depth), BF16),
            ],
            in_specs=[hbm] * 7,
            out_specs=[hbm] * 4,
            scratch_shapes=[
                pltpu.VMEM((tokens, depth), BF16),
                pltpu.VMEM((tokens, depth), BF16),
                pltpu.VMEM((tokens, hidden), BF16),
                pltpu.VMEM((tokens, hidden), BF16),
                pltpu.VMEM((tokens, hidden), BF16),
                pltpu.VMEM((depth, hidden), BF16),
                pltpu.VMEM((depth, hidden), BF16),
                pltpu.VMEM((hidden, depth), BF16),
                pltpu.VMEM((tokens, depth), BF16),
                pltpu.VMEM((RINGS, n, rows, cols), BF16),
                pltpu.VMEM((2, TILE, 2 * hidden), BF16),
                dma((3, n)),
                dma((CHUNKS,)),
                dma((2, RINGS)),
                dma,
                dma((2, 2)),
                dma,
                dma((RINGS,)),
                dma((RINGS, n)),
                dma((RINGS, n)),
            ],
            compiler_params=pltpu.CompilerParams(
                collective_id=0,
                has_side_effects=True,
                vmem_limit_bytes=67_043_328,
                fuse_transposed_lhs_in_matmul=True,
            ),
            cost_estimate=pl.CostEstimate(
                flops=12 * tokens * depth * hidden, bytes_accessed=14 * tokens * depth * 2, transcendentals=0
            ),
        )(x, dy, gate, up, w_gate, w_up, w_down)

    tokens, columns, rows = P("dp", None), P(None, "tp"), P("tp", None)
    return jax.shard_map(
        step,
        mesh=mesh,
        in_specs=(tokens, tokens, P("dp", "tp"), P("dp", "tp"), columns, columns, rows),
        out_specs=(tokens, P("dp", "tp"), P("dp", "tp"), P(("dp", "tp"), None)),
        check_vma=False,
    )
```

time: 261 us -> 205 us (0.79)
  Pallas kernels: 0 us -> 186 us
  waiting for transfers between devices: 126 us -> 0 us
  matrix products: 99.1 us -> 0 us
  between operations: 14.1 us -> 0.65 us
  local copies, waits for them, and re-layouts: 21.2 us -> 18 us
    pallas_call x0 -> x1, Pallas kernels: none -> 186 us  [step(): pl.pallas_call(functools.partial(kernel, n), name='mlp_backward', out_sha...]
    psum x1 -> x0, waiting for transfers between devices: 126 us -> none  [step(): dx = lax.psum(term.astype(jnp.bfloat16), 'tp')]
    dot_general x6 -> x0, matrix products: 99.1 us -> none  [the longest x1 20.5 us: step(): jnp.dot(d_up, w_up.T, preferred_element_type=jnp.float32)]
    unnamed x7 -> x10, local copies, waits for them, and re-layouts: 21.2 us -> 18 us
  transfers between devices with their start and end apart: 1 -> 0, of which waited for: 1 -> 0; matrix products, arithmetic and copies ran while one was open for 23% -> 0% of each run, Pallas kernels for 0% -> 0%
where the time goes in v1:
time: 205 us; the launch traced here: 204 us
  Pallas kernels  186 us (91%)
  local copies, waits for them, and re-layouts  18 us (9%)
    pallas_call x1, Pallas kernels, step(): pl.pallas_call(functools.partial(kernel, n), name='mlp_backward', out_sha...  186 us
    unnamed x10, local copies, waits for them, and re-layouts  18 us

profile of v1, /device:TPU:21, one launch (start us, length us, event | category | flops | bytes accessed | tf_op | source)
XLA Modules:
  0.0 204.4 jit_solution(10361468127165260591)
XLA Ops:
  0.6 185.7 %mlp_backward.1 = (bf16[2048,2048]{1,0:T(8,128)(2,1)}, bf16[2048,1024]{1,0:T(8,128)(2,1)}, bf16[2048,1024]{1,0:T(8,128)(2,1)}, bf16[1024,2048]{1,0:T(8,128)(2,1)}) custom-call(bf16[2048,2048]{1,0:T(8,128)(2,1)} %x.1, bf16[2048,2048]{1,0:T(8,128)(2,1)} %dy.1, bf16[2048,1024]{1,0:T(8,128)(2,1)} %gate.1, bf16[2048,1024]{1,0:T(8,128)(2,1)} %up.1, ...), custom_call_target="tpu_custom_call" | custom-call | flops 51539607552 | bytes 117440512 | tf_op jit(solution)/shard_map/mlp_backward/pallas_call | solution.py:345
  186.4 0.0 copy-start.2
  186.4 8.6 %copy.15 = bf16[2048,2048]{1,0:T(8,128)(2,1)} copy(bf16[2048,2048]{1,0:T(8,128)(2,1)} %get-tuple-element.8) | data formatting | bytes 16777216
  195.0 0.0 copy-done.2
  195.0 0.0 copy-start.1
  195.0 2.1 %copy.16 = bf16[2048,1024]{1,0:T(8,128)(2,1)} copy(bf16[2048,1024]{1,0:T(8,128)(2,1)S(1)} %copy-done.2) | data formatting | bytes 8388608
  197.1 1.6 copy-done.1
  198.7 0.0 copy-start
  198.7 2.1 %copy.17 = bf16[2048,1024]{1,0:T(8,128)(2,1)} copy(bf16[2048,1024]{1,0:T(8,128)(2,1)S(1)} %copy-done.1) | data formatting | bytes 8388608
  200.8 1.6 copy-done
  202.4 2.0 copy.18
Async XLA Ops:
  186.4 8.6 %copy-start.2 = (bf16[2048,1024]{1,0:T(8,128)(2,1)S(1)}, bf16[2048,1024]{1,0:T(8,128)(2,1)}, u32[]{:S(2)}) copy-start(bf16[2048,1024]{1,0:T(8,128)(2,1)} %get-tuple-element.9) | copy-start | bytes 12582916
  195.0 3.7 %copy-start.1 = (bf16[2048,1024]{1,0:T(8,128)(2,1)S(1)}, bf16[2048,1024]{1,0:T(8,128)(2,1)}, u32[]{:S(2)}) copy-start(bf16[2048,1024]{1,0:T(8,128)(2,1)} %get-tuple-element.10) | copy-start | bytes 12582916
  198.7 3.7 %copy-start = (bf16[1024,2048]{1,0:T(8,128)(2,1)S(1)}, bf16[1024,2048]{1,0:T(8,128)(2,1)}, u32[]{:S(2)}) copy-start(bf16[1024,2048]{1,0:T(8,128)(2,1)} %get-tuple-element.11) | copy-start | bytes 12582916

commit v2 on v1

--- a/solution.py
+++ b/solution.py
@@ -28,7 +28,6 @@
     dw_gate,
     dw_up,
     dw_down,
-    x_v,
     dy_v,
     dg_v,
     du_v,
@@ -36,15 +35,11 @@
     wg_v,
     wu_v,
     wd_v,
-    dx_v,
     slots,
-    stage,
     in_sem,
     wd_sem,
     w_sem,
     x_sem,
-    stage_sem,
-    dx_sem,
     send_sem,
     rs_sem,
     ag_sem,
@@ -86,7 +81,12 @@
             for k, (src, dst) in enumerate(((w_gate, wg_v), (w_up, wu_v)))
         ]
 
-    x_in = pltpu.make_async_copy(x, x_v, x_sem)
+    halves = [(wg_v, 0), (wu_v, hidden)]
+
+    def x_in(k):
+        dst, first = halves[k]
+        return pltpu.make_async_copy(x.at[:, pl.ds(first, hidden)], dst, x_sem.at[k])
+
 
     def right_block(t):
         return lax.rem(me + 2 * n - 1 - t, n)
@@ -111,7 +111,6 @@
 
     for copy in rows_in(left_block(n // 2)):
         copy.start()
-    x_in.start()
 
     def grads(b, c):
         at = (block(b), chunk(c))
@@ -145,7 +144,7 @@
         return lax.rem(me + n - 2 + t, n) if odd else lax.rem(me + n - t, n)
 
     def ag_copy(s, odd, t):
-        here = dx_v.at[block(ag_block(odd, t)), strip(s)]
+        here = dx.at[block(ag_block(odd, t)), strip(s)]
         return pltpu.make_async_remote_copy(
             src_ref=here,
             dst_ref=here,
@@ -155,10 +154,6 @@
             device_id_type=pl.DeviceIdType.MESH,
         )
 
-    def dx_out(s, odd, t):
-        at = (block(ag_block(odd, t)), strip(s))
-        return pltpu.make_async_copy(dx_v.at[at], dx.at[at], dx_sem)
-
     def send_first(s, odd):
         slots[s, 0] = term(right_block(0), s).astype(BF16)
         rs_copy(s, odd, 0).start()
@@ -174,16 +169,15 @@
         t = n - 1
         rs_copy(s, odd, t - 1).wait_recv()
         b = left_block(t) if odd else right_block(t)
-        dx_v[block(b), strip(s)] = (slots[s, t].astype(F32) + term(b, s)).astype(BF16)
+        dx[block(b), strip(s)] = (slots[s, t].astype(F32) + term(b, s)).astype(BF16)
         rs_copy(s, odd, t - 1).wait_send()
         ag_copy(s, odd, 0).start()
-        dx_out(s, odd, 0).start()
 
     def hand_on(s, odd, t, last=False):
         before = t - 1
         arrived = pltpu.make_async_remote_copy(
-            src_ref=dx_v.at[block(ag_block(odd, t)), strip(s)],
-            dst_ref=dx_v.at[block(ag_block(odd, t)), strip(s)],
+            src_ref=dx.at[block(ag_block(odd, t)), strip(s)],
+            dst_ref=dx.at[block(ag_block(odd, t)), strip(s)],
             send_sem=send_sem.at[s],
             recv_sem=ag_sem.at[s, before],
             device_id=target(odd),
@@ -193,42 +187,16 @@
         arrived.wait_send()
         if not last:
             ag_copy(s, odd, t).start()
-        dx_out(s, odd, t).start()
-
-    def stage_copies(i, slot, targets):
-        width = stage.shape[-1] // len(targets)
-        return [
-            pltpu.make_async_copy(
-                stage.at[slot, :, pl.ds(k * width, width)], dst.at[tile(i), :], stage_sem.at[k, slot]
-            )
-            for k, dst in enumerate(targets)
-        ]
 
     def down_grad(i):
-        slot = lax.rem(i, 2)
-
-        @pl.when(i >= 2)
-        def _():
-            for copy in stage_copies(i - 2, slot, [dw_down]):
-                copy.wait()
-
-        stage[slot] = lax.dot_general(hid_v[:, tile(i)], dy_v[...], TN, preferred_element_type=F32).astype(BF16)
-        for copy in stage_copies(i, slot, [dw_down]):
-            copy.start()
-
-    def up_grads(i):
-        slot = lax.rem(i, 2)
-
-        @pl.when(i >= 2)
-        def _():
-            for copy in stage_copies(i - 2, slot, [dw_gate, dw_up]):
-                copy.wait()
-
-        xt = x_v[:, tile(i)]
-        stage[slot, :, :hidden] = lax.dot_general(xt, dg_v[...], TN, preferred_element_type=F32).astype(BF16)
-        stage[slot, :, hidden:] = lax.dot_general(xt, du_v[...], TN, preferred_element_type=F32).astype(BF16)
-        for copy in stage_copies(i, slot, [dw_gate, dw_up]):
-            copy.start()
+        dw_down[tile(i), :] = lax.dot_general(hid_v[:, tile(i)], dy_v[...], TN, preferred_element_type=F32).astype(BF16)
+
+    def up_grads(k, i):
+        held, first = halves[k]
+        xt = held[:, tile(i)]
+        at = pl.ds(pl.multiple_of(first + i * TILE, TILE), TILE)
+        dw_gate[at, :] = lax.dot_general(xt, dg_v[...], TN, preferred_element_type=F32).astype(BF16)
+        dw_up[at, :] = lax.dot_general(xt, du_v[...], TN, preferred_element_type=F32).astype(BF16)
 
     for copy in rows_in(right_block(0)):
         copy.wait()
@@ -299,38 +267,45 @@
             def _():
                 down_grad(i)
 
-    for i in range(hidden // TILE - 2, hidden // TILE):
-        for copy in stage_copies(i, i % 2, [dw_down]):
-            copy.wait()
-    x_in.wait()
-
     @pl.loop(0, pairs)
     def _(j):
         finish(2 * j, 0)
         finish(2 * j + 1, 1)
 
-    @pl.loop(1, n - 1)
-    def _(t):
+    for k in range(2):
+        x_in(k).start()
+
+    def hand_on_all(t, last=False, also=None):
         @pl.loop(0, pairs)
         def _(j):
-            hand_on(2 * j, 0, t)
-            hand_on(2 * j + 1, 1, t)
-            i = (t - 1) * pairs + j
-
-            @pl.when(i < depth // TILE)
-            def _():
-                up_grads(i)
-
-    for i in range(depth // TILE - 2, depth // TILE):
-        for copy in stage_copies(i, i % 2, [dw_gate, dw_up]):
-            copy.wait()
-
-    @pl.loop(0, pairs)
-    def _(j):
-        hand_on(2 * j, 0, n - 1, last=True)
-        hand_on(2 * j + 1, 1, n - 1, last=True)
-
-    pltpu.make_async_copy(dx_v, dx, dx_sem).wait()
+            hand_on(2 * j, 0, t, last)
+            hand_on(2 * j + 1, 1, t, last)
+            if also is not None:
+                also(j)
+
+    hand_on_all(1)
+    steps = hidden // TILE // pairs
+    for k in range(2):
+        x_in(k).wait()
+
+        @pl.loop(0, steps)
+        def _(t):
+            hand_on_all(2 + k * steps + t, also=lambda j: up_grads(k, t * pairs + j))
+
+    @pl.loop(2 + 2 * steps, n - 1)
+    def _(t):
+        hand_on_all(t)
+
+    hand_on_all(n - 1, last=True)
+
+
+def write_out(*refs):
+    sources, targets, sem = refs[:4], refs[4:8], refs[8]
+    copies = [pltpu.make_async_copy(src, dst, sem.at[k]) for k, (src, dst) in enumerate(zip(sources, targets))]
+    for copy in copies:
+        copy.start()
+    for copy in copies:
+        copy.wait()
 
 
 def solution(mesh):
@@ -342,19 +317,15 @@
         rows, cols = tokens // n, depth // RINGS
         hbm = pl.BlockSpec(memory_space=pltpu.HBM)
         dma = pltpu.SemaphoreType.DMA
-        return pl.pallas_call(
+        shapes = [(tokens, depth), (depth, hidden), (depth, hidden), (hidden, depth)]
+        vmem = pl.BlockSpec(memory_space=pltpu.VMEM)
+        held = pl.pallas_call(
             functools.partial(kernel, n),
             name="mlp_backward",
-            out_shape=[
-                jax.ShapeDtypeStruct((tokens, depth), BF16),
-                jax.ShapeDtypeStruct((depth, hidden), BF16),
-                jax.ShapeDtypeStruct((depth, hidden), BF16),
-                jax.ShapeDtypeStruct((hidden, depth), BF16),
-            ],
+            out_shape=[pltpu.VMEM(shape, BF16) for shape in shapes],
             in_specs=[hbm] * 7,
-            out_specs=[hbm] * 4,
+            out_specs=[vmem] * 4,
             scratch_shapes=[
-                pltpu.VMEM((tokens, depth), BF16),
                 pltpu.VMEM((tokens, depth), BF16),
                 pltpu.VMEM((tokens, hidden), BF16),
                 pltpu.VMEM((tokens, hidden), BF16),
@@ -362,29 +333,31 @@
                 pltpu.VMEM((depth, hidden), BF16),
                 pltpu.VMEM((depth, hidden), BF16),
                 pltpu.VMEM((hidden, depth), BF16),
-                pltpu.VMEM((tokens, depth), BF16),
                 pltpu.VMEM((RINGS, n, rows, cols), BF16),
-                pltpu.VMEM((2, TILE, 2 * hidden), BF16),
                 dma((3, n)),
                 dma((CHUNKS,)),
                 dma((2, RINGS)),
-                dma,
-                dma((2, 2)),
-                dma,
+                dma((2,)),
                 dma((RINGS,)),
                 dma((RINGS, n)),
                 dma((RINGS, n)),
             ],
             compiler_params=pltpu.CompilerParams(
-                collective_id=0,
-                has_side_effects=True,
-                vmem_limit_bytes=67_043_328,
-                fuse_transposed_lhs_in_matmul=True,
+                collective_id=0, has_side_effects=True, vmem_limit_bytes=45_000_000
             ),
             cost_estimate=pl.CostEstimate(
                 flops=12 * tokens * depth * hidden, bytes_accessed=14 * tokens * depth * 2, transcendentals=0
             ),
         )(x, dy, gate, up, w_gate, w_up, w_down)
+        return pl.pallas_call(
+            write_out,
+            name="write_out",
+            out_shape=[jax.ShapeDtypeStruct(shape, BF16) for shape in shapes],
+            in_specs=[vmem] * 4,
+            out_specs=[hbm] * 4,
+            scratch_shapes=[dma((4,))],
+            compiler_params=pltpu.CompilerParams(vmem_limit_bytes=1_000_000),
+        )(*held)
 
     tokens, columns, rows = P("dp", None), P(None, "tp"), P("tp", None)
     return jax.shard_map(

time: 205 us -> 181 us (0.88)
  local copies, waits for them, and re-layouts: 18 us -> 0 us
  Pallas kernels: 186 us -> 180 us
    unnamed x10 -> x0, local copies, waits for them, and re-layouts: 18 us -> none
    pallas_call x1, Pallas kernels: 186 us -> 173 us  [step(): pl.pallas_call(functools.partial(kernel, n), name='mlp_backward', out_sha...]
    pallas_call x0 -> x1, Pallas kernels: none -> 7.33 us  [step(): pl.pallas_call(write_out, name='write_out', out_shape=[jax.ShapeDtypeStru...]
where the time goes in v2:
time: 181 us
  Pallas kernels  180 us (99%)
    pallas_call x1, Pallas kernels, step(): pl.pallas_call(functools.partial(kernel, n), name='mlp_backward', out_sha...  173 us
    pallas_call x1, Pallas kernels, step(): pl.pallas_call(write_out, name='write_out', out_shape=[jax.ShapeDtypeStru...  7.33 us

profile of v2, /device:TPU:21, one launch (start us, length us, event | category | flops | bytes accessed | tf_op | source)
XLA Modules:
  0.0 180.8 jit_solution(12545901559391761460)
XLA Ops:
  0.6 172.8 %mlp_backward.1 = (bf16[2048,2048]{1,0:T(8,128)(2,1)S(1)}, bf16[2048,1024]{1,0:T(8,128)(2,1)S(1)}, bf16[2048,1024]{1,0:T(8,128)(2,1)S(1)}, bf16[1024,2048]{1,0:T(8,128)(2,1)S(1)}) custom-call(bf16[2048,2048]{1,0:T(8,128)(2,1)} %x.1, bf16[2048,2048]{1,0:T(8,128)(2,1)} %dy.1, bf16[2048,1024]{1,0:T(8,128)(2,1)} %gate.1, bf16[2048,1024]{1,0:T(8,128)(2,1)} %up.1, ...), custom_call_target="tpu_custom_call" | custom-call | flops 51539607552 | bytes 117440512 | tf_op jit(solution)/shard_map/mlp_backward/pallas_call | solution.py:322
  173.4 7.3 %write_out.1 = (bf16[2048,2048]{1,0:T(8,128)(2,1)}, bf16[2048,1024]{1,0:T(8,128)(2,1)}, bf16[2048,1024]{1,0:T(8,128)(2,1)}, bf16[1024,2048]{1,0:T(8,128)(2,1)}) custom-call(bf16[2048,2048]{1,0:T(8,128)(2,1)S(1)} %get-tuple-element.8.refs_0_, bf16[2048,1024]{1,0:T(8,128)(2,1)S(1)} %get-tuple-element.9.refs_1_, ...), custom_call_target="tpu_custom_call" | custom-call | tf_op jit(solution)/shard_map/write_out/pallas_call | solution.py:352

commit v3 on v2

--- a/solution.py
+++ b/solution.py
@@ -25,6 +25,8 @@
     w_up,
     w_down,
     dx,
+    tail_right,
+    tail_left,
     dw_gate,
     dw_up,
     dw_down,
@@ -99,9 +101,11 @@
     for c in range(CHUNKS):
         down_in(c).start()
 
-    @pl.loop(0, RINGS)
-    def _(s):
-        for copy in strips_in(s):
+    pairs = RINGS // 2
+
+    @pl.loop(0, pairs)
+    def _(j):
+        for copy in strips_in(j) + strips_in(pairs + j):
             copy.start()
 
     @pl.loop(1, n // 2)
@@ -141,18 +145,26 @@
         )
 
     def ag_block(odd, t):
-        return lax.rem(me + n - 2 + t, n) if odd else lax.rem(me + n - t, n)
+        return gather_block(n, me, odd, t)
 
     def ag_copy(s, odd, t):
         here = dx.at[block(ag_block(odd, t)), strip(s)]
+        return ag_to(s, odd, t, here, here)
+
+    def ag_to(s, odd, t, src, dst):
         return pltpu.make_async_remote_copy(
-            src_ref=here,
-            dst_ref=here,
+            src_ref=src,
+            dst_ref=dst,
             send_sem=send_sem.at[s],
             recv_sem=ag_sem.at[s, t],
             device_id=target(odd),
             device_id_type=pl.DeviceIdType.MESH,
         )
+
+    def ag_last_copy(s, odd):
+        t = n - 3
+        dst = (tail_left if odd else tail_right).at[:, strip(s - odd * pairs)]
+        return ag_to(s, odd, t, dx.at[block(ag_block(odd, t)), strip(s)], dst)
 
     def send_first(s, odd):
         slots[s, 0] = term(right_block(0), s).astype(BF16)
@@ -173,20 +185,19 @@
         rs_copy(s, odd, t - 1).wait_send()
         ag_copy(s, odd, 0).start()
 
-    def hand_on(s, odd, t, last=False):
-        before = t - 1
-        arrived = pltpu.make_async_remote_copy(
-            src_ref=dx.at[block(ag_block(odd, t)), strip(s)],
-            dst_ref=dx.at[block(ag_block(odd, t)), strip(s)],
-            send_sem=send_sem.at[s],
-            recv_sem=ag_sem.at[s, before],
-            device_id=target(odd),
-            device_id_type=pl.DeviceIdType.MESH,
-        )
+    def hand_on(s, odd, t):
+        here = dx.at[block(ag_block(odd, t)), strip(s)]
+        arrived = ag_to(s, odd, t - 1, here, here)
         arrived.wait_recv()
         arrived.wait_send()
-        if not last:
+
+        @pl.when(t < n - 3)
+        def _():
             ag_copy(s, odd, t).start()
+
+        @pl.when(t == n - 3)
+        def _():
+            ag_last_copy(s, odd).start()
 
     def down_grad(i):
         dw_down[tile(i), :] = lax.dot_general(hid_v[:, tile(i)], dy_v[...], TN, preferred_element_type=F32).astype(BF16)
@@ -207,15 +218,13 @@
         grads(right_block(0), c)
 
     pl.semaphore_wait(barrier, 2)
-    pairs = RINGS // 2
-    per_pair = 2 * CHUNKS // pairs
 
     @pl.loop(0, pairs)
     def _(j):
         for odd in range(2):
-            for copy in strips_in(2 * j + odd):
+            for copy in strips_in(odd * pairs + j):
                 copy.wait()
-            send_first(2 * j + odd, odd)
+            send_first(odd * pairs + j, odd)
 
     def arrive(b):
         for copy in rows_in(b):
@@ -242,25 +251,25 @@
 
         @pl.loop(0, pairs)
         def _(j):
-            pass_on(2 * j, 0, t)
+            pass_on(j, 0, t)
             grads(right_block(t + 1), j)
-            pass_on(2 * j + 1, 1, t)
+            pass_on(pairs + j, 1, t)
             grads(left_block(t + 1), j)
 
     arrive(left_block(half))
 
     @pl.loop(0, pairs)
     def _(j):
-        pass_on(2 * j, 0, half - 1)
+        pass_on(j, 0, half - 1)
         grads(left_block(half), j)
-        pass_on(2 * j + 1, 1, half - 1)
+        pass_on(pairs + j, 1, half - 1)
 
     @pl.loop(half, n - 1)
     def _(t):
         @pl.loop(0, pairs)
         def _(j):
-            pass_on(2 * j, 0, t)
-            pass_on(2 * j + 1, 1, t)
+            pass_on(j, 0, t)
+            pass_on(pairs + j, 1, t)
             i = (t - half) * pairs + j
 
             @pl.when(i < hidden // TILE)
@@ -269,17 +278,17 @@
 
     @pl.loop(0, pairs)
     def _(j):
-        finish(2 * j, 0)
-        finish(2 * j + 1, 1)
+        finish(j, 0)
+        finish(pairs + j, 1)
 
     for k in range(2):
         x_in(k).start()
 
-    def hand_on_all(t, last=False, also=None):
+    def hand_on_all(t, also=None):
         @pl.loop(0, pairs)
         def _(j):
-            hand_on(2 * j, 0, t, last)
-            hand_on(2 * j + 1, 1, t, last)
+            hand_on(j, 0, t)
+            hand_on(pairs + j, 1, t)
             if also is not None:
                 also(j)
 
@@ -292,20 +301,42 @@
         def _(t):
             hand_on_all(2 + k * steps + t, also=lambda j: up_grads(k, t * pairs + j))
 
-    @pl.loop(2 + 2 * steps, n - 1)
-    def _(t):
-        hand_on_all(t)
-
-    hand_on_all(n - 1, last=True)
-
-
-def write_out(*refs):
-    sources, targets, sem = refs[:4], refs[4:8], refs[8]
-    copies = [pltpu.make_async_copy(src, dst, sem.at[k]) for k, (src, dst) in enumerate(zip(sources, targets))]
+    @pl.loop(0, pairs)
+    def _(j):
+        for odd in range(2):
+            last = ag_last_copy(odd * pairs + j, odd)
+            last.wait_recv()
+            last.wait_send()
+
+
+def gather_block(n, me, odd, t):
+    return lax.rem(me + n - 2 + t, n) if odd else lax.rem(me + n - t, n)
+
+
+def move(pairs_of_refs, sem):
+    copies = [pltpu.make_async_copy(src, dst, sem.at[k]) for k, (src, dst) in enumerate(pairs_of_refs)]
     for copy in copies:
         copy.start()
     for copy in copies:
         copy.wait()
+
+
+def place(n, ref, odd, t):
+    rows, cols = ref.shape[0] // n, ref.shape[1] // 2
+    b = gather_block(n, lax.axis_index("tp"), odd, t)
+    return ref.at[pl.ds(pl.multiple_of(b * rows, rows), rows), pl.ds(odd * cols, cols)]
+
+
+def write_out(n, dx_v, tail_right, tail_left, dw_gate_v, dw_up_v, dw_down_v, dx, dw_gate, dw_up, dw_down, sem):
+    moves = [(dw_gate_v, dw_gate), (dw_up_v, dw_up), (dw_down_v, dw_down)]
+    for odd, tail in enumerate((tail_right, tail_left)):
+        moves += [(place(n, dx_v, odd, t), place(n, dx, odd, t)) for t in range(n - 2)]
+        moves.append((tail, place(n, dx, odd, n - 2)))
+    move(moves, sem)
+
+
+def put_last(n, _, from_left, from_right, dx, sem):
+    move([(from_left, place(n, dx, 0, n - 1)), (from_right, place(n, dx, 1, n - 1))], sem)
 
 
 def solution(mesh):
@@ -318,13 +349,14 @@
         hbm = pl.BlockSpec(memory_space=pltpu.HBM)
         dma = pltpu.SemaphoreType.DMA
         shapes = [(tokens, depth), (depth, hidden), (depth, hidden), (hidden, depth)]
+        tail = (rows, depth // 2)
         vmem = pl.BlockSpec(memory_space=pltpu.VMEM)
         held = pl.pallas_call(
             functools.partial(kernel, n),
             name="mlp_backward",
-            out_shape=[pltpu.VMEM(shape, BF16) for shape in shapes],
+            out_shape=[pltpu.VMEM(shape, BF16) for shape in (shapes[0], tail, tail, *shapes[1:])],
             in_specs=[hbm] * 7,
-            out_specs=[vmem] * 4,
+            out_specs=[vmem] * 6,
             scratch_shapes=[
                 pltpu.VMEM((tokens, depth), BF16),
                 pltpu.VMEM((tokens, hidden), BF16),
@@ -343,21 +375,38 @@
                 dma((RINGS, n)),
             ],
             compiler_params=pltpu.CompilerParams(
-                collective_id=0, has_side_effects=True, vmem_limit_bytes=45_000_000
+                collective_id=0, has_side_effects=True, vmem_limit_bytes=44_500_000
             ),
             cost_estimate=pl.CostEstimate(
                 flops=12 * tokens * depth * hidden, bytes_accessed=14 * tokens * depth * 2, transcendentals=0
             ),
         )(x, dy, gate, up, w_gate, w_up, w_down)
-        return pl.pallas_call(
-            write_out,
+        around = range(n)
+        from_left = lax.ppermute(held[1], "tp", [(i, (i + 1) % n) for i in around])
+        from_right = lax.ppermute(held[2], "tp", [(i, (i - 1) % n) for i in around])
+        dx, *grads = pl.pallas_call(
+            functools.partial(write_out, n),
             name="write_out",
             out_shape=[jax.ShapeDtypeStruct(shape, BF16) for shape in shapes],
-            in_specs=[vmem] * 4,
+            in_specs=[vmem] * 6,
             out_specs=[hbm] * 4,
-            scratch_shapes=[dma((4,))],
+            scratch_shapes=[dma((2 * n + 1,))],
             compiler_params=pltpu.CompilerParams(vmem_limit_bytes=1_000_000),
+            cost_estimate=pl.CostEstimate(
+                flops=tokens * depth * hidden, bytes_accessed=5 * tokens * depth * 2, transcendentals=0
+            ),
         )(*held)
+        dx = pl.pallas_call(
+            functools.partial(put_last, n),
+            name="put_last",
+            out_shape=jax.ShapeDtypeStruct(shapes[0], BF16),
+            in_specs=[hbm, vmem, vmem],
+            out_specs=hbm,
+            input_output_aliases={0: 0},
+            scratch_shapes=[dma((2,))],
+            compiler_params=pltpu.CompilerParams(vmem_limit_bytes=1_000_000),
+        )(dx, from_left, from_right)
+        return dx, *grads
 
     tokens, columns, rows = P("dp", None), P(None, "tp"), P("tp", None)
     return jax.shard_map(

time: 181 us -> 178 us (0.983)
  Pallas kernels: 180 us -> 169 us
  waiting for transfers between devices: 0 us -> 4.31 us
  starting transfers between devices: 0 us -> 2.76 us
    pallas_call x1, Pallas kernels: 173 us -> 162 us  [step(): pl.pallas_call(functools.partial(kernel, n), name='mlp_backward', out_sha...]
    ppermute x0 -> x2, waiting for transfers between devices: none -> 4.31 us  [the longest x1 4.3 us: step(): from_left = lax.ppermute(held[1], 'tp', [(i, (i + 1) % n) for i in around])]
    ppermute x0 -> x2, starting transfers between devices: none -> 2.76 us  [the longest x1 2.65 us: step(): from_right = lax.ppermute(held[2], 'tp', [(i, (i - 1) % n) for i in around])]
    pallas_call x1 -> x2, Pallas kernels: 7.33 us -> 7.87 us  [the longest x1 6.89 us: step(): pl.pallas_call(functools.partial(write_out, n), name='write_out', out_sha...]
  transfers between devices with their start and end apart: 0 -> 2, of which waited for: 0 -> 1; matrix products, arithmetic and copies ran while one was open for 0% -> 0% of each run, Pallas kernels for 0% -> 4%
where the time goes in v3:
time: 178 us; the launch traced here: 177 us
  Pallas kernels  169 us (95%)
  waiting for transfers between devices  4.31 us (2%)
  starting transfers between devices  2.76 us (2%)
    pallas_call x1, Pallas kernels, step(): pl.pallas_call(functools.partial(kernel, n), name='mlp_backward', out_sha...  162 us
    pallas_call x1, Pallas kernels, step(): pl.pallas_call(functools.partial(write_out, n), name='write_out', out_sha...  6.89 us
    ppermute x1, waiting for transfers between devices, step(): from_left = lax.ppermute(held[1], 'tp', [(i, (i + 1) % n) for i in around])  4.3 us
  transfers between devices with their start and end apart: 2, of which 1 were waited for; matrix products, arithmetic and copies ran while one was open for 0% of the time, Pallas kernels for 4%

profile of v3, /device:TPU:21, one launch (start us, length us, event | category | flops | bytes accessed | tf_op | source)
XLA Modules:
  0.0 177.2 jit_solution(17312949785375138387)
XLA Ops:
  0.6 161.6 %mlp_backward.1 = (bf16[2048,2048]{1,0:T(8,128)(2,1)S(1)}, bf16[256,1024]{1,0:T(8,128)(2,1)S(1)}, bf16[256,1024]{1,0:T(8,128)(2,1)S(1)}, bf16[2048,1024]{1,0:T(8...) custom-call(bf16[2048,2048]{1,0:T(8,128)(2,1)} %x.1, bf16[2048,2048]{1,0:T(8,128)(2,1)} %dy.1, ...), custom_call_target="tpu_custom_call" | custom-call | flops 51539607552 | bytes 117440512 | tf_op jit(solution)/shard_map/mlp_backward/pallas_call | solution.py:354
  162.2 0.1 collective-permute-start
  162.3 2.6 %collective-permute-start.1 = (bf16[256,1024]{1,0:T(8,128)(2,1)S(1)}, bf16[256,1024]{1,0:T(8,128)(2,1)S(1)}, u32[]{:S(2)}, u32[]{:S(2)}) collective-permute-start(bf16[256,1024]{1,0:T(8,128)(2,1)S(1)} %get-tuple-element.16.tail_left), channel_id=1, source_target_pairs={{0,7},{1,0},{2,1},{3,2},{4,3},{5,4},{6,5},{7,6},{8,15},{9,8},{10,9... | collective-permute-start | bytes 1572872 | tf_op jit(solution)/shard_map/ppermute | solution.py:386
  165.0 6.9 %write_out.1 = (bf16[2048,2048]{1,0:T(8,128)(2,1)}, bf16[2048,1024]{1,0:T(8,128)(2,1)}, bf16[2048,1024]{1,0:T(8,128)(2,1)}, bf16[1024,2048]{1,0:T(8,128)(2,1)}) custom-call(bf16[2048,2048]{1,0:T(8,128)(2,1)S(1)} %get-tuple-element.14.dx_v, bf16[256,1024]{1,0:T(8,128)(2,1)S(1)} %get-tuple-element.15.tail_right, ...), custom_call_target="tpu_custom_call" | custom-call | flops 4294967296 | bytes 41943040 | tf_op jit(solution)/shard_map/write_out/pallas_call | solution.py:387
  171.9 4.3 %collective-permute-done.from_left = bf16[256,1024]{1,0:T(8,128)(2,1)S(1)} collective-permute-done((bf16[256,1024]{1,0:T(8,128)(2,1)S(1)}, bf16[256,1024]{1,0:T(8,128)(2,1)S(1)}, u32[]{:S(2)}, u32[]{:S(2)}) %collective-permute-start) | collective-permute-done | bytes 524320 | tf_op jit(solution)/shard_map/ppermute | solution.py:385
  176.2 0.0 collective-permute-done.1.from_right
  176.2 1.0 put_last.1
Async XLA Ops:
  162.2 14.0 %collective-permute-start = (bf16[256,1024]{1,0:T(8,128)(2,1)S(1)}, bf16[256,1024]{1,0:T(8,128)(2,1)S(1)}, u32[]{:S(2)}, u32[]{:S(2)}) collective-permute-start(bf16[256,1024]{1,0:T(8,128)(2,1)S(1)} %get-tuple-element.15.tail_right), channel_id=1, source_target_pairs={{0,1},{1,2},{2,3},{3,4},{4,5},{5,6},{6,7},{7,0},{8,9},{9,10},{10,1... | collective-permute-start | bytes 1572872 | tf_op jit(solution)/shard_map/ppermute | solution.py:385
  162.3 13.9 %collective-permute-start.1 = (bf16[256,1024]{1,0:T(8,128)(2,1)S(1)}, bf16[256,1024]{1,0:T(8,128)(2,1)S(1)}, u32[]{:S(2)}, u32[]{:S(2)}) collective-permute-start(bf16[256,1024]{1,0:T(8,128)(2,1)S(1)} %get-tuple-element.16.tail_left), channel_id=1, source_target_pairs={{0,7},{1,0},{2,1},{3,2},{4,3},{5,4},{6,5},{7,6},{8,15},{9,8},{10,9... | collective-permute-start | bytes 1572872 | tf_op jit(solution)/shard_map/ppermute | solution.py:386

commit v4 on v3

--- a/solution.py
+++ b/solution.py
@@ -71,7 +71,7 @@
     def rows_in(b):
         return [
             pltpu.make_async_copy(src.at[block(b), :], dst.at[block(b), :], in_sem.at[k, b])
-            for k, (src, dst) in enumerate(((dy, dy_v), (gate, dg_v), (up, du_v)))
+            for k, (src, dst) in enumerate(((gate, dg_v), (up, du_v), (dy, dy_v)))
         ]
 
     def down_in(c):
@@ -96,25 +96,26 @@
     def left_block(t):
         return lax.rem(me + n - 1 + t, n)
 
-    for copy in rows_in(right_block(0)):
+    first = rows_in(right_block(0))
+    for copy in first:
         copy.start()
-    for c in range(CHUNKS):
-        down_in(c).start()
+    down_in(0).start()
 
     pairs = RINGS // 2
 
-    @pl.loop(0, pairs)
-    def _(j):
-        for copy in strips_in(j) + strips_in(pairs + j):
+    def start_rest():
+        @pl.loop(0, pairs)
+        def _(j):
+            for copy in strips_in(j) + strips_in(pairs + j):
+                copy.start()
+
+        @pl.loop(1, n // 2)
+        def _(t):
+            for copy in rows_in(right_block(t)) + rows_in(left_block(t)):
+                copy.start()
+
+        for copy in rows_in(left_block(n // 2)):
             copy.start()
-
-    @pl.loop(1, n // 2)
-    def _(t):
-        for copy in rows_in(right_block(t)) + rows_in(left_block(t)):
-            copy.start()
-
-    for copy in rows_in(left_block(n // 2)):
-        copy.start()
 
     def grads(b, c):
         at = (block(b), chunk(c))
@@ -209,8 +210,14 @@
         dw_gate[at, :] = lax.dot_general(xt, dg_v[...], TN, preferred_element_type=F32).astype(BF16)
         dw_up[at, :] = lax.dot_general(xt, du_v[...], TN, preferred_element_type=F32).astype(BF16)
 
-    for copy in rows_in(right_block(0)):
-        copy.wait()
+    down_in(1).start()
+    first[0].wait()
+    down_in(2).start()
+    first[1].wait()
+    down_in(3).start()
+
+    start_rest()
+    first[2].wait()
 
     @pl.loop(0, CHUNKS)
     def _(c):

time: 178 us -> 177 us (level)
  no operation moved by 1% of the time
where the time goes in v4:
time: 177 us
  Pallas kernels  169 us (95%)
  waiting for transfers between devices  4.31 us (2%)
  starting transfers between devices  2.76 us (2%)
    pallas_call x1, Pallas kernels, step(): pl.pallas_call(functools.partial(kernel, n), name='mlp_backward', out_sha...  161 us
    pallas_call x1, Pallas kernels, step(): pl.pallas_call(functools.partial(write_out, n), name='write_out', out_sha...  6.89 us
    ppermute x1, waiting for transfers between devices, step(): from_left = lax.ppermute(held[1], 'tp', [(i, (i + 1) % n) for i in around])  4.3 us
  transfers between devices with their start and end apart: 2, of which 1 were waited for; matrix products, arithmetic and copies ran while one was open for 0% of the time, Pallas kernels for 4%

profile of v4, /device:TPU:21, one launch (start us, length us, event | category | flops | bytes accessed | tf_op | source)
XLA Modules:
  0.0 176.6 jit_solution(8188990603650844151)
XLA Ops:
  0.6 161.0 %mlp_backward.1 = (bf16[2048,2048]{1,0:T(8,128)(2,1)S(1)}, bf16[256,1024]{1,0:T(8,128)(2,1)S(1)}, bf16[256,1024]{1,0:T(8,128)(2,1)S(1)}, bf16[2048,1024]{1,0:T(8...) custom-call(bf16[2048,2048]{1,0:T(8,128)(2,1)} %x.1, bf16[2048,2048]{1,0:T(8,128)(2,1)} %dy.1, ...), custom_call_target="tpu_custom_call" | custom-call | flops 51539607552 | bytes 117440512 | tf_op jit(solution)/shard_map/mlp_backward/pallas_call | solution.py:361
  161.6 0.1 collective-permute-start
  161.7 2.6 %collective-permute-start.1 = (bf16[256,1024]{1,0:T(8,128)(2,1)S(1)}, bf16[256,1024]{1,0:T(8,128)(2,1)S(1)}, u32[]{:S(2)}, u32[]{:S(2)}) collective-permute-start(bf16[256,1024]{1,0:T(8,128)(2,1)S(1)} %get-tuple-element.16.tail_left), channel_id=1, source_target_pairs={{0,7},{1,0},{2,1},{3,2},{4,3},{5,4},{6,5},{7,6},{8,15},{9,8},{10,9... | collective-permute-start | bytes 1572872 | tf_op jit(solution)/shard_map/ppermute | solution.py:393
  164.4 6.9 %write_out.1 = (bf16[2048,2048]{1,0:T(8,128)(2,1)}, bf16[2048,1024]{1,0:T(8,128)(2,1)}, bf16[2048,1024]{1,0:T(8,128)(2,1)}, bf16[1024,2048]{1,0:T(8,128)(2,1)}) custom-call(bf16[2048,2048]{1,0:T(8,128)(2,1)S(1)} %get-tuple-element.14.dx_v, bf16[256,1024]{1,0:T(8,128)(2,1)S(1)} %get-tuple-element.15.tail_right, ...), custom_call_target="tpu_custom_call" | custom-call | flops 4294967296 | bytes 41943040 | tf_op jit(solution)/shard_map/write_out/pallas_call | solution.py:394
  171.3 4.3 %collective-permute-done.from_left = bf16[256,1024]{1,0:T(8,128)(2,1)S(1)} collective-permute-done((bf16[256,1024]{1,0:T(8,128)(2,1)S(1)}, bf16[256,1024]{1,0:T(8,128)(2,1)S(1)}, u32[]{:S(2)}, u32[]{:S(2)}) %collective-permute-start) | collective-permute-done | bytes 524320 | tf_op jit(solution)/shard_map/ppermute | solution.py:392
  175.6 0.0 collective-permute-done.1.from_right
  175.6 1.0 put_last.1
Async XLA Ops:
  161.6 14.0 %collective-permute-start = (bf16[256,1024]{1,0:T(8,128)(2,1)S(1)}, bf16[256,1024]{1,0:T(8,128)(2,1)S(1)}, u32[]{:S(2)}, u32[]{:S(2)}) collective-permute-start(bf16[256,1024]{1,0:T(8,128)(2,1)S(1)} %get-tuple-element.15.tail_right), channel_id=1, source_target_pairs={{0,1},{1,2},{2,3},{3,4},{4,5},{5,6},{6,7},{7,0},{8,9},{9,10},{10,1... | collective-permute-start | bytes 1572872 | tf_op jit(solution)/shard_map/ppermute | solution.py:392
  161.7 13.9 %collective-permute-start.1 = (bf16[256,1024]{1,0:T(8,128)(2,1)S(1)}, bf16[256,1024]{1,0:T(8,128)(2,1)S(1)}, u32[]{:S(2)}, u32[]{:S(2)}) collective-permute-start(bf16[256,1024]{1,0:T(8,128)(2,1)S(1)} %get-tuple-element.16.tail_left), channel_id=1, source_target_pairs={{0,7},{1,0},{2,1},{3,2},{4,3},{5,4},{6,5},{7,6},{8,15},{9,8},{10,9... | collective-permute-start | bytes 1572872 | tf_op jit(solution)/shard_map/ppermute | solution.py:393

commit v5 on v4

--- a/solution.py
+++ b/solution.py
@@ -7,7 +7,7 @@
 from jax.experimental.pallas import tpu as pltpu
 from jax.sharding import PartitionSpec as P
 
-RINGS = 8
+RINGS = 4
 CHUNKS = 4
 TILE = 128
 BF16, F32 = jnp.bfloat16, jnp.float32
@@ -259,16 +259,19 @@
         @pl.loop(0, pairs)
         def _(j):
             pass_on(j, 0, t)
-            grads(right_block(t + 1), j)
+            for c in range(CHUNKS // pairs):
+                grads(right_block(t + 1), j * (CHUNKS // pairs) + c)
             pass_on(pairs + j, 1, t)
-            grads(left_block(t + 1), j)
+            for c in range(CHUNKS // pairs):
+                grads(left_block(t + 1), j * (CHUNKS // pairs) + c)
 
     arrive(left_block(half))
 
     @pl.loop(0, pairs)
     def _(j):
         pass_on(j, 0, half - 1)
-        grads(left_block(half), j)
+        for c in range(CHUNKS // pairs):
+            grads(left_block(half), j * (CHUNKS // pairs) + c)
         pass_on(pairs + j, 1, half - 1)
 
     @pl.loop(half, n - 1)
@@ -279,9 +282,10 @@
             pass_on(pairs + j, 1, t)
             i = (t - half) * pairs + j
 
-            @pl.when(i < hidden // TILE)
+            @pl.when(i < hidden // TILE // 2)
             def _():
-                down_grad(i)
+                down_grad(2 * i)
+                down_grad(2 * i + 1)
 
     @pl.loop(0, pairs)
     def _(j):
@@ -300,13 +304,13 @@
                 also(j)
 
     hand_on_all(1)
-    steps = hidden // TILE // pairs
+    steps = hidden // TILE // pairs // 2
     for k in range(2):
         x_in(k).wait()
 
         @pl.loop(0, steps)
         def _(t):
-            hand_on_all(2 + k * steps + t, also=lambda j: up_grads(k, t * pairs + j))
+            hand_on_all(2 + k * steps + t, also=lambda j: [up_grads(k, 2 * (t * pairs + j) + q) for q in range(2)])
 
     @pl.loop(0, pairs)
     def _(j):

time: 177 us -> 176 us (level)
  no operation moved by 1% of the time
where the time goes in v5:
time: 176 us; the launch traced here: 175 us
  Pallas kernels  168 us (95%)
  waiting for transfers between devices  3.94 us (2%)
  starting transfers between devices  2.76 us (2%)
    pallas_call x1, Pallas kernels, step(): pl.pallas_call(functools.partial(kernel, n), name='mlp_backward', out_sha...  160 us
    pallas_call x1, Pallas kernels, step(): pl.pallas_call(functools.partial(write_out, n), name='write_out', out_sha...  6.89 us
    ppermute x1, waiting for transfers between devices, step(): from_left = lax.ppermute(held[1], 'tp', [(i, (i + 1) % n) for i in around])  3.94 us
  transfers between devices with their start and end apart: 2, of which 1 were waited for; matrix products, arithmetic and copies ran while one was open for 0% of the time, Pallas kernels for 4%

profile of v5, /device:TPU:21, one launch (start us, length us, event | category | flops | bytes accessed | tf_op | source)
XLA Modules:
  0.0 175.3 jit_solution(7116648779981418288)
XLA Ops:
  0.6 159.9 %mlp_backward.1 = (bf16[2048,2048]{1,0:T(8,128)(2,1)S(1)}, bf16[256,1024]{1,0:T(8,128)(2,1)S(1)}, bf16[256,1024]{1,0:T(8,128)(2,1)S(1)}, bf16[2048,1024]{1,0:T(8...) custom-call(bf16[2048,2048]{1,0:T(8,128)(2,1)} %x.1, bf16[2048,2048]{1,0:T(8,128)(2,1)} %dy.1, ...), custom_call_target="tpu_custom_call" | custom-call | flops 51539607552 | bytes 117440512 | tf_op jit(solution)/shard_map/mlp_backward/pallas_call | solution.py:365
  160.6 0.1 collective-permute-start
  160.7 2.6 %collective-permute-start.1 = (bf16[256,1024]{1,0:T(8,128)(2,1)S(1)}, bf16[256,1024]{1,0:T(8,128)(2,1)S(1)}, u32[]{:S(2)}, u32[]{:S(2)}) collective-permute-start(bf16[256,1024]{1,0:T(8,128)(2,1)S(1)} %get-tuple-element.16.tail_left), channel_id=1, source_target_pairs={{0,7},{1,0},{2,1},{3,2},{4,3},{5,4},{6,5},{7,6},{8,15},{9,8},{10,9... | collective-permute-start | bytes 1572872 | tf_op jit(solution)/shard_map/ppermute | solution.py:397
  163.4 6.9 %write_out.1 = (bf16[2048,2048]{1,0:T(8,128)(2,1)}, bf16[2048,1024]{1,0:T(8,128)(2,1)}, bf16[2048,1024]{1,0:T(8,128)(2,1)}, bf16[1024,2048]{1,0:T(8,128)(2,1)}) custom-call(bf16[2048,2048]{1,0:T(8,128)(2,1)S(1)} %get-tuple-element.14.dx_v, bf16[256,1024]{1,0:T(8,128)(2,1)S(1)} %get-tuple-element.15.tail_right, ...), custom_call_target="tpu_custom_call" | custom-call | flops 4294967296 | bytes 41943040 | tf_op jit(solution)/shard_map/write_out/pallas_call | solution.py:398
  170.3 3.9 %collective-permute-done.from_left = bf16[256,1024]{1,0:T(8,128)(2,1)S(1)} collective-permute-done((bf16[256,1024]{1,0:T(8,128)(2,1)S(1)}, bf16[256,1024]{1,0:T(8,128)(2,1)S(1)}, u32[]{:S(2)}, u32[]{:S(2)}) %collective-permute-start) | collective-permute-done | bytes 524320 | tf_op jit(solution)/shard_map/ppermute | solution.py:396
  174.2 0.0 collective-permute-done.1.from_right
  174.2 1.0 put_last.1
Async XLA Ops:
  160.6 13.6 %collective-permute-start = (bf16[256,1024]{1,0:T(8,128)(2,1)S(1)}, bf16[256,1024]{1,0:T(8,128)(2,1)S(1)}, u32[]{:S(2)}, u32[]{:S(2)}) collective-permute-start(bf16[256,1024]{1,0:T(8,128)(2,1)S(1)} %get-tuple-element.15.tail_right), channel_id=1, source_target_pairs={{0,1},{1,2},{2,3},{3,4},{4,5},{5,6},{6,7},{7,0},{8,9},{9,10},{10,1... | collective-permute-start | bytes 1572872 | tf_op jit(solution)/shard_map/ppermute | solution.py:396
  160.7 13.5 %collective-permute-start.1 = (bf16[256,1024]{1,0:T(8,128)(2,1)S(1)}, bf16[256,1024]{1,0:T(8,128)(2,1)S(1)}, u32[]{:S(2)}, u32[]{:S(2)}) collective-permute-start(bf16[256,1024]{1,0:T(8,128)(2,1)S(1)} %get-tuple-element.16.tail_left), channel_id=1, source_target_pairs={{0,7},{1,0},{2,1},{3,2},{4,3},{5,4},{6,5},{7,6},{8,15},{9,8},{10,9... | collective-permute-start | bytes 1572872 | tf_op jit(solution)/shard_map/ppermute | solution.py:397
